TPU v7x, 32 devices: a whole 2x2x4 slice. The times are simulated.
32 devices in a mesh: track: 4 (over y, x), ifg: 4 (over z), pix: 2 (over core).
Axes of the slice: x: 2, y: 2, z: 4, core: 2. Of those that a mesh axis runs over, the one named last changes fastest.
Arguments:
- phases: bfloat16 [4, 600, 32768], P('track', 'ifg', 'pix')
- pairs: int32 [4, 600, 2], P('track', 'ifg'), may hold values from 0 to 249, as said below
- date_map: int32 [4, 250], replicated, may hold values from 0 to 319, as said below
- knots: int32 [32], replicated, may hold values from 0 to 319, as said below
- look: float32 [4, 3, 32768], P(None, None, 'pix'), may hold values from -1 to 1
Outputs:
- enu: float32 [3, 320, 32768], P(None, None, ('pix', 'ifg', 'track'))
- spline: float32 [3, 32, 32768], P(None, None, ('pix', 'ifg', 'track'))
Inputs may be any that keep to these rules, and one draw needn't show every extreme that they name: pairs[t, k, 0] < pairs[t, k, 1] <= pairs[t, k, 0] + 5. `date_map`: the dates of one track map to distinct epochs. `knots`: strictly increasing, the first 0 and the last 319.
All inputs are finite; a program needn't handle non-finite values.
Results may differ from a plain program's by a relative error of at most 0.0003.
Values may be sent and summed in bfloat16 or wider, within the bound.
A program may use at most 128 MiB of HBM per device.

v0:
```python
import jax
import jax.numpy as jnp
from jax import lax
from jax.sharding import PartitionSpec as P

EPOCHS = 320
damping = 0.5
ridge = 0.1
HIGH = lax.Precision.HIGHEST


def incidence(pair_rows, ndate):
    dates = jnp.arange(ndate, dtype=jnp.int32)[:, None]
    later = (dates == pair_rows[None, :, 1]).astype(jnp.float32)
    earlier = (dates == pair_rows[None, :, 0]).astype(jnp.float32)
    return later - earlier


def inverse_normal(normal_part):
    ndate = normal_part.shape[0]
    normal = normal_part + damping * jnp.eye(ndate, dtype=jnp.float32)
    factor = jnp.linalg.cholesky(normal)
    return jax.scipy.linalg.cho_solve((factor, True), jnp.eye(ndate, dtype=jnp.float32))


def hat_basis(knots, n_epochs):
    spots = knots.astype(jnp.float32)
    left = jnp.concatenate([spots[:1] - 1.0, spots[:-1]])
    right = jnp.concatenate([spots[1:], spots[-1:] + 1.0])
    epochs = jnp.arange(n_epochs, dtype=jnp.float32)[:, None]
    rise = (epochs - left) / (spots - left)
    fall = (right - epochs) / (right - spots)
    return jnp.maximum(0.0, jnp.minimum(rise, fall))


def geometry(series, date_map, look, knots, n_epochs):
    epochs = jnp.arange(n_epochs, dtype=jnp.int32)
    onehot = (date_map[:, None, :] == epochs[None, :, None]).astype(jnp.float32)
    seen = jnp.sum(onehot, axis=2)
    resampled = jnp.einsum("tcd,tdp->tcp", onehot, series, precision=HIGH)

    def entry(first, second):
        value = jnp.einsum("tc,tp->cp", seen, look[:, first] * look[:, second], precision=HIGH)
        if first == second:
            value = value + ridge
        return value

    a00, a01, a02 = (entry(0, 0), entry(0, 1), entry(0, 2))
    a11, a12, a22 = (entry(1, 1), entry(1, 2), entry(2, 2))
    b_all = [jnp.sum(look[:, i][:, None, :] * resampled, axis=0) for i in range(3)]
    c00 = a11 * a22 - a12 * a12
    c01 = a02 * a12 - a01 * a22
    c02 = a01 * a12 - a02 * a11
    c11 = a00 * a22 - a02 * a02
    c12 = a01 * a02 - a00 * a12
    c22 = a00 * a11 - a01 * a01
    det = a00 * c00 + a01 * c01 + a02 * c02
    east = (c00 * b_all[0] + c01 * b_all[1] + c02 * b_all[2]) / det
    north = (c01 * b_all[0] + c11 * b_all[1] + c12 * b_all[2]) / det
    upward = (c02 * b_all[0] + c12 * b_all[1] + c22 * b_all[2]) / det
    enu = jnp.stack([east, north, upward])
    basis = hat_basis(knots, n_epochs)
    gram = jnp.dot(basis.T, basis, precision=HIGH)
    factor = jnp.linalg.cholesky(gram)
    fitter = jax.scipy.linalg.cho_solve((factor, True), basis.T)
    spline = jnp.einsum("kc,icp->ikp", fitter, enu, precision=HIGH)
    return (enu, spline)


def shards(phases, pairs, date_map, knots, look):
    ndate = date_map.shape[1]
    n_epochs = hat_count()
    n_track = lax.axis_size("track")
    n_ifg = lax.axis_size("ifg")
    width = phases.shape[2] // (n_track * n_ifg)
    offset = lax.axis_index("ifg") * (width * n_track) + lax.axis_index("track") * width
    look_local = lax.dynamic_slice_in_dim(look, offset, width, 2)
    phase_rows = phases[0]
    pair_rows = pairs[0]
    phase_all = lax.all_to_all(phase_rows, "ifg", split_axis=1, concat_axis=0, tiled=True)
    pair_all = lax.all_gather(pair_rows, "ifg", axis=0, tiled=True)
    incid = incidence(pair_all, ndate)
    normal_part = jnp.dot(incid, incid.T, precision=HIGH)
    rhs = jnp.dot(incid.astype(jnp.bfloat16), phase_all, preferred_element_type=jnp.float32)
    ninv = inverse_normal(normal_part)
    pixel_count = rhs.shape[1] * lax.axis_size("ifg") * lax.axis_size("pix")
    series = jnp.dot(ninv, rhs, precision=HIGH)
    total = lax.psum(jnp.sum(series, axis=1), ("ifg", "pix"))
    series = series - (total / pixel_count)[:, None]
    gathered = lax.all_to_all(series[None], "track", split_axis=2, concat_axis=0, tiled=True)
    return geometry(gathered, date_map, look_local, knots, n_epochs)


def hat_count():
    return EPOCHS


def solution(mesh):
    in_specs = (P("track", "ifg", "pix"), P("track", "ifg", None), P(), P(), P(None, None, "pix"))
    out_specs = (P(None, None, ("pix", "ifg", "track")), P(None, None, ("pix", "ifg", "track")))
    return jax.shard_map(shards, mesh=mesh, in_specs=in_specs, out_specs=out_specs, check_vma=False)
```

profile of v0, /device:TPU:0, one launch (start us, length us, event | category | flops | bytes accessed | tf_op | source)
XLA Modules:
  0.0 324.4 jit_solution(3422282366233087118)
XLA Ops:
  0.6 11.1 %all_to_all.27 = bf16[150,4,4096]{2,1,0:T(4,128)(2,1)} reshape(bf16[1,150,16384]{2,1,0:T(8,128)(2,1)} %param.5) | data formatting | bytes 9830400 | tf_op jit(solution)/shard_map/all_to_all | solution.py:80
  11.7 7.3 %copy.23 = bf16[150,4,4096]{2,0,1:T(8,128)(2,1)} copy(bf16[150,4,4096]{2,1,0:T(4,128)(2,1)} %all_to_all.27) | data formatting | bytes 9830400 | tf_op jit(solution)/shard_map/all_to_all | solution.py:80
  19.1 6.5 %all-to-all-start = ((bf16[150,4,4096]{2,0,1:T(8,128)(2,1)}), bf16[150,4,4096]{2,0,1:T(8,128)(2,1)}, u32[]{:S(2)}, u32[]{:S(2)}) async-start(bf16[150,4,4096]{2,0,1:T(8,128)(2,1)} %copy.23), calls=%async_computation | async-start | bytes 9961472 | tf_op jit(solution)/shard_map/all_to_all | solution.py:80
  25.6 0.0 copy-done.5
  25.6 0.1 copy.21
  25.7 118.2 %all-gather = s32[1,600,2]{2,0,1:T(1,128)S(1)} all-gather(s32[1,150,2]{2,0,1:T(1,128)S(1)} %copy.21), channel_id=2, replica_groups=mesh['track'=4,'ifg'=4,'pix'=2] {'ifg'}, dimensions={1}, use_global_device_ids=true | all-gather | bytes 6000 | tf_op jit(solution)/shard_map/all_gather | solution.py:81
  143.9 0.3 slice_reduce_fusion.1
  144.3 1.0 fusion.3
  145.3 0.1 copy.22
  145.5 0.1 fusion.16
  145.5 0.0 copy-start.6
  145.5 11.7 %cholesky.63 = f32[128,128]{1,0:T(8,128)S(1)} custom-call(f32[128,128]{1,0:T(8,128)S(1)} %cholesky.156), custom_call_target="Cholesky" | custom-call | tf_op jit(solution)/shard_map/jit(cholesky)/cholesky | solution.py:22
  157.3 9.8 %custom-call.28 = f32[1,128,128]{1,2,0:T(8,128)S(1)} custom-call(f32[1,128,128]{2,1,0:T(8,128)S(1)} %get-tuple-element.40), custom_call_target="InvertDiagBlocksLowerTriangular" | custom-call | tf_op jit(solution)/shard_map/jit(cholesky)/cholesky | solution.py:22
  167.1 0.2 constant_dynamic-update-slice_fusion
  167.3 0.3 convolution_subtract_fusion.2
  167.6 11.2 %cholesky.133 = f32[122,122]{1,0:T(8,128)S(1)} custom-call(f32[122,122]{1,0:T(8,128)S(1)} %convolution_subtract_fusion.2), custom_call_target="Cholesky" | custom-call | tf_op jit(solution)/shard_map/jit(cholesky)/cholesky | solution.py:22
  178.8 0.6 compare_reduce_fusion.1
  179.5 0.6 compare_reduce_fusion.2
  181.5 0.1 fusion.21
  181.6 20.2 %custom-call.29 = f32[2,128,128]{1,2,0:T(8,128)S(1)} custom-call(f32[2,128,128]{2,1,0:T(8,128)S(1)} %pad_maximum_fusion.1), custom_call_target="InvertDiagBlocksLowerTriangular" | custom-call | tf_op jit(solution)/shard_map/jit(_cho_solve)/triangular_solve | solution.py:23
  201.8 0.0 copy-done.6
  201.9 0.1 fusion.47
  201.9 0.3 fusion.17
  202.2 0.3 convolution_subtract_fusion.1
  202.5 0.3 fusion.27
  202.8 0.3 fusion.26
  203.0 0.3 convolution_subtract_fusion
  203.4 0.3 fusion.25
  203.6 0.0 all-to-all-done
  203.6 6.0 %all_to_all.30 = bf16[600,4096]{1,0:T(8,128)(2,1)} reshape(bf16[4,150,4096]{2,1,0:T(8,128)(2,1)} %bitcast.11) | data formatting | bytes 9830400 | tf_op jit(solution)/shard_map/all_to_all | solution.py:80
  209.6 4.2 %fusion.5 = f32[250,4096]{1,0:T(8,128)S(1)} fusion(bf16[600,4096]{1,0:T(8,128)(2,1)} %all_to_all.30, s32[600]{0:T(1024)S(1)} %get-tuple-element.26, s32[600]{0:T(1024)S(1)} %get-tuple-element.25), kind=kOutput, calls=%fused_computation.31 | convolution fusion | flops 1229699968 | bytes 9016000 | tf_op jit(solution)/shard_map/dot_general | solution.py:84
  213.8 5.3 %fusion.48 = (f32[250]{0:T(256)S(1)}, f32[250,4096]{1,0:T(8,128)}) fusion(f32[250,4096]{1,0:T(8,128)S(1)} %fusion.5, f32[122,250]{1,0:T(8,128)S(1)} %fusion.26, f32[128,250]{1,0:T(8,128)S(1)} %fusion.25), kind=kOutput, calls=%fused_computation.113 | convolution fusion | flops 3073086208 | bytes 8443000 | tf_op jit(solution)/shard_map/dot_general | solution.py:87
  219.1 13.6 %psum.7 = f32[250]{0:T(256)S(1)} all-reduce(f32[250]{0:T(256)S(1)} %get-tuple-element.49), channel_id=1, replica_groups=mesh['track'=4,'ifg'=4,'pix'=2] {'ifg','pix'}, use_global_device_ids=true, to_apply=%region_6.7 | all-reduce | flops 250 | bytes 2000 | tf_op jit(solution)/shard_map/psum | solution.py:88
  232.7 4.7 %subtract_bitcast_fusion = f32[1,250,4096]{2,1,0:T(8,128)} fusion(f32[250,4096]{1,0:T(8,128)} %get-tuple-element.50, f32[250]{0:T(256)S(1)} %broadcast_multiply_fusion), kind=kLoop, calls=%fused_computation.5 | loop fusion | flops 1024000 | bytes 8193000 | tf_op jit(solution)/shard_map/broadcast_in_dim | solution.py:90
  237.4 10.2 %copy.24 = f32[1,250,4096]{1,0,2:T(1,128)} copy(f32[1,250,4096]{2,1,0:T(8,128)} %subtract_bitcast_fusion) | data formatting | bytes 8192000 | tf_op jit(solution)/shard_map/broadcast_in_dim | solution.py:90
  247.6 5.0 %all-to-all-start.1 = ((f32[1,250,4096]{1,0,2:T(1,128)}), f32[1,250,4096]{1,0,2:T(1,128)}, u32[]{:S(2)}, u32[]{:S(2)}) async-start(f32[1,250,4096]{1,0,2:T(1,128)} %copy.24), calls=%async_computation.1 | async-start | bytes 8388608 | tf_op jit(solution)/shard_map/all_to_all | solution.py:90
  252.6 0.6 fusion.46
  254.5 0.1 convert_subtract_fusion.3
  254.6 0.4 fusion.20
  255.1 0.1 copy.26
  255.1 2.9 cholesky.147
  258.1 0.6 compare_reduce_fusion
  258.7 0.7 fusion.30
  259.4 2.4 custom-call.30
  261.8 0.8 dynamic-slice_bitcast_fusion.2
  262.6 0.3 fusion.19
  263.0 0.2 convolution_bitcast_fusion.1
  263.2 0.0 copy-done.4
  263.2 0.3 convert_reduce_fusion
  263.5 2.4 convolution_add_fusion
  265.8 2.4 convolution_add_fusion.1
  268.2 2.3 convolution_add_fusion.2
  270.5 1.2 fusion.35
  271.8 1.3 fusion.37
  273.0 27.3 %all-to-all-done.1 = f32[1,250,4096]{1,0,2:T(1,128)} async-done(((f32[1,250,4096]{1,0,2:T(1,128)}), f32[1,250,4096]{1,0,2:T(1,128)}, u32[]{:S(2)}, u32[]{:S(2)}) %all-to-all-start.1) | async-done | bytes 4096032 | tf_op jit(solution)/shard_map/all_to_all | solution.py:90
  300.3 4.4 %copy.27 = f32[1,250,4096]{1,2,0:T(8,128)} copy(f32[1,250,4096]{1,0,2:T(1,128)} %all-to-all-done.1) | data formatting | bytes 8192000
  304.8 5.6 %copy.25 = f32[1,250,4,1024]{3,1,2,0:T(8,128)} copy(f32[1,250,4,1024]{1,3,2,0:T(8,128)} %bitcast.82) | data formatting | bytes 8192000 | tf_op jit(solution)/shard_map/all_to_all | solution.py:90
  310.4 0.0 copy-start.3
  310.4 6.9 %multiply_reduce_fusion.2 = (f32[320,1024]{1,0:T(8,128)S(1)}, f32[320,1024]{1,0:T(8,128)S(1)}, f32[320,1024]{1,0:T(8,128)S(1)}) fusion(f32[4,1024]{1,0:T(4,128)S(1)} %get-tuple-element.36, f32[4,1024]{1,0:T(4,128)S(1)} %get-tuple-element.35, f32[4,1024]{1,0:T(4,128)S(1)} %get-tuple-element.34, f32[1,250,4,1024]{3,1,2,0:T(8,128)} %copy.25, ...), kind=kOutput, calls=%fused_computation.2 | convolution fusion | flops 3939361280 | bytes 8081312 | tf_op jit(solution)/shard_map/tcd,tdp->tcp/dot_general | solution.py:40
  317.3 3.0 divide_bitcast_fusion.2
  320.3 0.5 pad_maximum_fusion
  320.9 0.0 copy-start
  320.9 3.3 %convolution_bitcast_fusion = f32[3,32,1024]{2,1,0:T(8,128)} fusion(f32[3,320,1024]{2,1,0:T(8,128)S(1)} %pad_maximum_fusion, f32[32,320,1]{1,0,2:T(8,128)S(1)} %convolution_bitcast_fusion.1), kind=kOutput, calls=%fused_computation.20 | convolution fusion | flops 377487360 | bytes 4366336 | tf_op jit(solution)/shard_map/kc,icp->ikp/dot_general | solution.py:66
  324.2 0.0 copy-done
  (21 shorter events, 0.3 us)
Async XLA Ops:
  19.1 6.5 %copy-start.5 = (s32[1,150,2]{1,2,0:T(2,128)S(1)}, s32[1,150,2]{1,2,0:T(2,128)}, u32[]{:S(2)}) copy-start(s32[1,150,2]{1,2,0:T(2,128)} %param.6) | copy-start | bytes 3604
  19.1 184.6 %all-to-all-start = ((bf16[150,4,4096]{2,0,1:T(8,128)(2,1)}), bf16[150,4,4096]{2,0,1:T(8,128)(2,1)}, u32[]{:S(2)}, u32[]{:S(2)}) async-start(bf16[150,4,4096]{2,0,1:T(8,128)(2,1)} %copy.23), calls=%async_computation | async-start | bytes 9961472 | tf_op jit(solution)/shard_map/all_to_all | solution.py:80
  145.5 56.3 %copy-start.6 = (s32[32]{0:T(128)S(1)}, s32[32]{0:T(128)}, u32[]{:S(2)}) copy-start(s32[32]{0:T(128)} %param.8) | copy-start | bytes 388
  247.6 52.7 %all-to-all-start.1 = ((f32[1,250,4096]{1,0,2:T(1,128)}), f32[1,250,4096]{1,0,2:T(1,128)}, u32[]{:S(2)}, u32[]{:S(2)}) async-start(f32[1,250,4096]{1,0,2:T(1,128)} %copy.24), calls=%async_computation.1 | async-start | bytes 8388608 | tf_op jit(solution)/shard_map/all_to_all | solution.py:90
  254.6 8.6 %copy-start.4 = (s32[4,250]{1,0:T(4,128)S(1)}, s32[4,250]{1,0:T(4,128)}, u32[]{:S(2)}) copy-start(s32[4,250]{1,0:T(4,128)} %param.7) | copy-start | bytes 12004
  310.4 6.9 %copy-start.1 = (f32[320,1024]{1,0:T(8,128)S(1)}, f32[320,1024]{1,0:T(8,128)}, u32[]{:S(2)}) copy-start(f32[320,1024]{1,0:T(8,128)} %convolution_add_fusion) | copy-start | bytes 3932164
  310.4 6.9 %copy-start.2 = (f32[320,1024]{1,0:T(8,128)S(1)}, f32[320,1024]{1,0:T(8,128)}, u32[]{:S(2)}) copy-start(f32[320,1024]{1,0:T(8,128)} %convolution_add_fusion.1) | copy-start | bytes 3932164
  310.4 6.9 %copy-start.3 = (f32[320,1024]{1,0:T(8,128)S(1)}, f32[320,1024]{1,0:T(8,128)}, u32[]{:S(2)}) copy-start(f32[320,1024]{1,0:T(8,128)} %convolution_add_fusion.2) | copy-start | bytes 3932164
  320.9 3.3 %copy-start = (f32[3,320,1024]{2,1,0:T(8,128)}, f32[3,320,1024]{2,1,0:T(8,128)S(1)}, u32[]{:S(2)}) copy-start(f32[3,320,1024]{2,1,0:T(8,128)S(1)} %pad_maximum_fusion) | copy-start | bytes 11796484
where the time goes:
time: 329 us; the launch traced here: 324 us
  blocking collectives  132 us (40%)
  other arithmetic  66.8 us (20%)
  local copies, waits for them, and re-layouts  46.8 us (14%)
  matrix products  36.4 us (11%)
  waiting for transfers between devices  27.3 us (8%)
  starting transfers between devices  11.5 us (3%)
  between operations  3.84 us (1%)
    all_gather x1, blocking collectives, shards(): pair_all = lax.all_gather(pair_rows, 'ifg', axis=0, tiled=True)  118 us
    another operation x7, other arithmetic, inverse_normal(): factor = jnp.linalg.cholesky(normal)  34 us
    all_to_all x1, waiting for transfers between devices, shards(): lax.all_to_all(series[None], 'track', split_axis=2, concat_axis=0, tiled=...  27.3 us
    all_to_all x3, local copies, waits for them, and re-layouts, shards(): lax.all_to_all(phase_rows, 'ifg', split_axis=1, concat_axis=0, tiled=True)  24.4 us
    another operation x6, other arithmetic, inverse_normal(): jax.scipy.linalg.cho_solve((factor, True), jnp.eye(ndate, dtype=jnp.float...  20.3 us
    psum x1, blocking collectives, shards(): total = lax.psum(jnp.sum(series, axis=1), ('ifg', 'pix'))  13.6 us
    dot_general x6, matrix products, entry(): jnp.einsum('tc,tp->cp', seen, look[:, first] * look[:, second], precision...  12.6 us
    broadcast_in_dim x1, local copies, waits for them, and re-layouts, shards(): series[None]  10.2 us
  transfers between devices with their start and end apart: 2, of which 1 were waited for; matrix products, arithmetic and copies ran while one was open for 24% of the time, Pallas kernels for 0%

commit v1 on v0

--- a/solution.py
+++ b/solution.py
@@ -2,6 +2,7 @@
 import jax.numpy as jnp
 from jax import lax
 from jax.sharding import PartitionSpec as P
+from jax.lax import all_to_all, axis_size
 
 EPOCHS = 320
 damping = 0.5
@@ -87,7 +88,15 @@
     series = jnp.dot(ninv, rhs, precision=HIGH)
     total = lax.psum(jnp.sum(series, axis=1), ("ifg", "pix"))
     series = series - (total / pixel_count)[:, None]
-    gathered = lax.all_to_all(series[None], "track", split_axis=2, concat_axis=0, tiled=True)
+    gathered = jnp.concatenate(
+        all_to_all(
+            jnp.stack(jnp.split(series[None], axis_size("track"), axis=2), axis=0),
+            axis_name="track",
+            split_axis=0,
+            concat_axis=0,
+        ),
+        axis=0,
+    )
     return geometry(gathered, date_map, look_local, knots, n_epochs)
 
 

time: 329 us -> 312 us (0.948)
  local copies, waits for them, and re-layouts: 46.8 us -> 33.3 us
    broadcast_in_dim x1 -> x0, local copies, waits for them, and re-layouts: 10.2 us -> none  [shards(): series[None]]
    another operation x0 -> x2, local copies, waits for them, and re-layouts: none -> 6.7 us  [shards(): jnp.stack(jnp.split(series[None], axis_size('track'), axis=2), axis=0)]
    all_to_all x1 -> x0, local copies, waits for them, and re-layouts: 5.6 us -> none  [shards(): lax.all_to_all(series[None], 'track', split_axis=2, concat_axis=0, tiled=...]
    unnamed x16 -> x15, local copies, waits for them, and re-layouts: 4.58 us -> 0.15 us
  transfers between devices with their start and end apart: 2 -> 2, of which waited for: 1 -> 1; matrix products, arithmetic and copies ran while one was open for 24% -> 25% of each run, Pallas kernels for 0% -> 0%
where the time goes in v1:
time: 312 us; the launch traced here: 308 us
  blocking collectives  132 us (42%)
  other arithmetic  64.7 us (21%)
  matrix products  36.8 us (12%)
  local copies, waits for them, and re-layouts  33.3 us (11%)
  waiting for transfers between devices  26.1 us (8%)
  starting transfers between devices  11.5 us (4%)
  between operations  3.87 us (1%)
    all_gather x1, blocking collectives, shards(): pair_all = lax.all_gather(pair_rows, 'ifg', axis=0, tiled=True)  118 us
    another operation x7, other arithmetic, inverse_normal(): factor = jnp.linalg.cholesky(normal)  34 us
    all_to_all x1, waiting for transfers between devices, shards(): all_to_all(jnp.stack(jnp.split(series[None], axis_size('track'), axis=2),...  26.1 us
    all_to_all x3, local copies, waits for them, and re-layouts, shards(): lax.all_to_all(phase_rows, 'ifg', split_axis=1, concat_axis=0, tiled=True)  24.4 us
    another operation x6, other arithmetic, inverse_normal(): jax.scipy.linalg.cho_solve((factor, True), jnp.eye(ndate, dtype=jnp.float...  20 us
    psum x1, blocking collectives, shards(): total = lax.psum(jnp.sum(series, axis=1), ('ifg', 'pix'))  13.6 us
    dot_general x6, matrix products, entry(): jnp.einsum('tc,tp->cp', seen, look[:, first] * look[:, second], precision...  12.8 us
    dot_general x1, matrix products, geometry(): resampled = jnp.einsum('tcd,tdp->tcp', onehot, series, precision=HIGH)  7.12 us
  transfers between devices with their start and end apart: 2, of which 1 were waited for; matrix products, arithmetic and copies ran while one was open for 25% of the time, Pallas kernels for 0%

profile of v1, /device:TPU:0, one launch (start us, length us, event | category | flops | bytes accessed | tf_op | source)
XLA Modules:
  0.0 308.0 jit_solution(17866302643728049910)
XLA Ops:
  0.6 11.1 %all_to_all.17 = bf16[150,4,4096]{2,1,0:T(4,128)(2,1)} reshape(bf16[1,150,16384]{2,1,0:T(8,128)(2,1)} %param.5) | data formatting | bytes 9830400 | tf_op jit(solution)/shard_map/all_to_all | solution.py:81
  11.7 7.3 %copy.19 = bf16[150,4,4096]{2,0,1:T(8,128)(2,1)} copy(bf16[150,4,4096]{2,1,0:T(4,128)(2,1)} %all_to_all.17) | data formatting | bytes 9830400 | tf_op jit(solution)/shard_map/all_to_all | solution.py:81
  19.1 6.5 %all-to-all-start = ((bf16[150,4,4096]{2,0,1:T(8,128)(2,1)}), bf16[150,4,4096]{2,0,1:T(8,128)(2,1)}, u32[]{:S(2)}, u32[]{:S(2)}) async-start(bf16[150,4,4096]{2,0,1:T(8,128)(2,1)} %copy.19), calls=%async_computation | async-start | bytes 9961472 | tf_op jit(solution)/shard_map/all_to_all | solution.py:81
  25.6 0.0 copy-done.5
  25.6 0.1 copy.17
  25.7 118.2 %all-gather = s32[1,600,2]{2,0,1:T(1,128)S(1)} all-gather(s32[1,150,2]{2,0,1:T(1,128)S(1)} %copy.17), channel_id=2, replica_groups=mesh['track'=4,'ifg'=4,'pix'=2] {'ifg'}, dimensions={1}, use_global_device_ids=true | all-gather | bytes 6000 | tf_op jit(solution)/shard_map/all_gather | solution.py:82
  143.9 0.3 slice_reduce_fusion.1
  144.3 1.0 fusion.4
  145.3 0.1 copy.18
  145.5 0.1 fusion.17
  145.5 0.0 copy-start.6
  145.5 11.7 %cholesky.63 = f32[128,128]{1,0:T(8,128)S(1)} custom-call(f32[128,128]{1,0:T(8,128)S(1)} %cholesky.156), custom_call_target="Cholesky" | custom-call | tf_op jit(solution)/shard_map/jit(cholesky)/cholesky | solution.py:23
  157.3 9.8 %custom-call.28 = f32[1,128,128]{1,2,0:T(8,128)S(1)} custom-call(f32[1,128,128]{2,1,0:T(8,128)S(1)} %get-tuple-element.44), custom_call_target="InvertDiagBlocksLowerTriangular" | custom-call | tf_op jit(solution)/shard_map/jit(cholesky)/cholesky | solution.py:23
  167.1 0.2 constant_dynamic-update-slice_fusion
  167.3 0.3 convolution_subtract_fusion.2
  167.6 11.2 %cholesky.133 = f32[122,122]{1,0:T(8,128)S(1)} custom-call(f32[122,122]{1,0:T(8,128)S(1)} %convolution_subtract_fusion.2), custom_call_target="Cholesky" | custom-call | tf_op jit(solution)/shard_map/jit(cholesky)/cholesky | solution.py:23
  178.8 0.6 compare_reduce_fusion.1
  179.5 0.6 compare_reduce_fusion.2
  181.5 0.1 fusion.22
  181.6 19.8 %custom-call.29 = f32[2,128,128]{1,2,0:T(8,128)S(1)} custom-call(f32[2,128,128]{2,1,0:T(8,128)S(1)} %pad_maximum_fusion.2), custom_call_target="InvertDiagBlocksLowerTriangular" | custom-call | tf_op jit(solution)/shard_map/jit(_cho_solve)/triangular_solve | solution.py:24
  201.4 0.0 copy-done.6
  201.5 0.1 fusion.48
  201.6 0.3 fusion.18
  201.8 0.3 convolution_subtract_fusion.1
  202.1 0.3 fusion.28
  202.4 0.3 fusion.27
  202.7 0.3 convolution_subtract_fusion
  203.0 0.3 fusion.26
  203.3 0.0 all-to-all-done
  203.3 6.0 %all_to_all.20 = bf16[600,4096]{1,0:T(8,128)(2,1)} reshape(bf16[4,150,4096]{2,1,0:T(8,128)(2,1)} %bitcast.11) | data formatting | bytes 9830400 | tf_op jit(solution)/shard_map/all_to_all | solution.py:81
  209.2 4.2 %fusion.6 = f32[250,4096]{1,0:T(8,128)S(1)} fusion(bf16[600,4096]{1,0:T(8,128)(2,1)} %all_to_all.20, s32[600]{0:T(1024)S(1)} %get-tuple-element.26, s32[600]{0:T(1024)S(1)} %get-tuple-element.25), kind=kOutput, calls=%fused_computation.37 | convolution fusion | flops 1229699968 | bytes 9016000 | tf_op jit(solution)/shard_map/dot_general | solution.py:85
  213.5 5.3 %fusion.49 = (f32[250]{0:T(256)S(1)}, f32[250,4096]{1,0:T(8,128)}) fusion(f32[250,4096]{1,0:T(8,128)S(1)} %fusion.6, f32[122,250]{1,0:T(8,128)S(1)} %fusion.27, f32[128,250]{1,0:T(8,128)S(1)} %fusion.26), kind=kOutput, calls=%fused_computation.119 | convolution fusion | flops 3073086208 | bytes 8443000 | tf_op jit(solution)/shard_map/dot_general | solution.py:88
  218.7 13.6 %psum.7 = f32[250]{0:T(256)S(1)} all-reduce(f32[250]{0:T(256)S(1)} %get-tuple-element.53), channel_id=1, replica_groups=mesh['track'=4,'ifg'=4,'pix'=2] {'ifg','pix'}, use_global_device_ids=true, to_apply=%region_6.7 | all-reduce | flops 250 | bytes 2000 | tf_op jit(solution)/shard_map/psum | solution.py:89
  232.3 2.6 subtract_bitcast_fusion
  235.0 0.6 slice_bitcast_fusion.3
  235.5 0.3 pad_maximum_fusion
  235.9 6.1 %copy.20 = f32[4,1,250,1024]{3,1,2,0:T(1,128)} copy(f32[4,1,250,1024]{3,2,1,0:T(8,128)S(1)} %pad_maximum_fusion) | data formatting | bytes 8192000 | tf_op jit(solution)/shard_map/stack | solution.py:93
  242.0 5.0 %all-to-all-start.1 = ((f32[4,1,250,1024]{3,1,2,0:T(1,128)}), f32[4,1,250,1024]{3,1,2,0:T(1,128)}, u32[]{:S(2)}, u32[]{:S(2)}) async-start(f32[4,1,250,1024]{3,1,2,0:T(1,128)} %copy.20), calls=%async_computation.1 | async-start | bytes 8192000 | tf_op jit(solution)/shard_map/all_to_all | solution.py:92
  247.0 0.6 fusion.47
  248.9 0.1 convert_subtract_fusion.3
  249.0 0.4 fusion.21
  249.4 0.1 copy.21
  249.5 2.9 cholesky.147
  252.5 0.6 compare_reduce_fusion
  253.1 0.7 fusion.31
  253.8 2.4 custom-call.30
  256.2 0.8 dynamic-slice_bitcast_fusion.2
  257.0 0.3 fusion.20
  257.4 0.2 convolution_bitcast_fusion.1
  257.5 0.0 copy-done.4
  257.6 0.3 convert_reduce_fusion
  257.8 2.3 convolution_add_fusion
  260.2 2.4 convolution_add_fusion.1
  262.6 2.3 convolution_add_fusion.2
  264.9 1.2 fusion.36
  266.1 1.3 fusion.38
  267.4 26.1 %all-to-all-done.1 = f32[4,1,250,1024]{3,1,2,0:T(1,128)} async-done(((f32[4,1,250,1024]{3,1,2,0:T(1,128)}), f32[4,1,250,1024]{3,1,2,0:T(1,128)}, u32[]{:S(2)}, u32[]{:S(2)}) %all-to-all-start.1) | async-done | bytes 4096032 | tf_op jit(solution)/shard_map/all_to_all | solution.py:92
  293.5 7.1 %multiply_reduce_fusion.2 = (f32[320,1024]{1,0:T(8,128)S(1)}, f32[320,1024]{1,0:T(8,128)S(1)}, f32[320,1024]{1,0:T(8,128)S(1)}) fusion(f32[4,1024]{1,0:T(4,128)S(1)} %get-tuple-element.40, f32[4,1024]{1,0:T(4,128)S(1)} %get-tuple-element.39, f32[4,1024]{1,0:T(4,128)S(1)} %get-tuple-element.38, f32[4,1,250,1024]{3,1,2,0:T(1,128)} %all-to-all-done.1, ...), kind=kOutput, calls=%fused_computation.2 | convolution fusion | flops 3939361280 | bytes 8081312 | tf_op jit(solution)/shard_map/tcd,tdp->tcp/dot_general | solution.py:41
  300.6 0.0 copy-done.1
  300.6 0.0 copy-done.2
  300.6 3.3 %divide_bitcast_fusion.2 = (f32[1,320,1024]{2,1,0:T(8,128)S(1)}, f32[1,320,1024]{2,1,0:T(8,128)S(1)}, f32[1,320,1024]{2,1,0:T(8,128)S(1)}) fusion(f32[320,1024]{1,0:T(8,128)S(1)} %get-tuple-element.23, f32[320,1024]{1,0:T(8,128)S(1)} %get-tuple-element.24, f32[320,1024]{1,0:T(8,128)S(1)} %get-tuple-element.22, f32[320,1024]{1,0:T(8,128)S(1)} %copy-done.3, ...), kind=kOutput, calls=%fused_computation.15 | convolution fusion | flops 29167616 | bytes 14455808 | tf_op jit(solution)/shard_map/tc,tp->cp/dot_general | solution.py:44
  303.9 0.5 pad_maximum_fusion.1
  304.4 0.0 copy-start
  304.5 3.3 %convolution_bitcast_fusion = f32[3,32,1024]{2,1,0:T(8,128)} fusion(f32[3,320,1024]{2,1,0:T(8,128)S(1)} %pad_maximum_fusion.1, f32[32,320,1]{1,0,2:T(8,128)S(1)} %convolution_bitcast_fusion.1), kind=kOutput, calls=%fused_computation.22 | convolution fusion | flops 377487360 | bytes 4366336 | tf_op jit(solution)/shard_map/kc,icp->ikp/dot_general | solution.py:67
  (21 shorter events, 0.3 us)
Async XLA Ops:
  19.1 6.5 %copy-start.5 = (s32[1,150,2]{1,2,0:T(2,128)S(1)}, s32[1,150,2]{1,2,0:T(2,128)}, u32[]{:S(2)}) copy-start(s32[1,150,2]{1,2,0:T(2,128)} %param.6) | copy-start | bytes 3604
  19.1 184.2 %all-to-all-start = ((bf16[150,4,4096]{2,0,1:T(8,128)(2,1)}), bf16[150,4,4096]{2,0,1:T(8,128)(2,1)}, u32[]{:S(2)}, u32[]{:S(2)}) async-start(bf16[150,4,4096]{2,0,1:T(8,128)(2,1)} %copy.19), calls=%async_computation | async-start | bytes 9961472 | tf_op jit(solution)/shard_map/all_to_all | solution.py:81
  145.5 55.9 %copy-start.6 = (s32[32]{0:T(128)S(1)}, s32[32]{0:T(128)}, u32[]{:S(2)}) copy-start(s32[32]{0:T(128)} %param.8) | copy-start | bytes 388
  242.0 51.5 %all-to-all-start.1 = ((f32[4,1,250,1024]{3,1,2,0:T(1,128)}), f32[4,1,250,1024]{3,1,2,0:T(1,128)}, u32[]{:S(2)}, u32[]{:S(2)}) async-start(f32[4,1,250,1024]{3,1,2,0:T(1,128)} %copy.20), calls=%async_computation.1 | async-start | bytes 8192000 | tf_op jit(solution)/shard_map/all_to_all | solution.py:92
  249.0 8.6 %copy-start.4 = (s32[4,250]{1,0:T(4,128)S(1)}, s32[4,250]{1,0:T(4,128)}, u32[]{:S(2)}) copy-start(s32[4,250]{1,0:T(4,128)} %param.7) | copy-start | bytes 12004
  293.5 7.1 %copy-start.1 = (f32[320,1024]{1,0:T(8,128)S(1)}, f32[320,1024]{1,0:T(8,128)}, u32[]{:S(2)}) copy-start(f32[320,1024]{1,0:T(8,128)} %convolution_add_fusion) | copy-start | bytes 3932164
  293.5 7.1 %copy-start.2 = (f32[320,1024]{1,0:T(8,128)S(1)}, f32[320,1024]{1,0:T(8,128)}, u32[]{:S(2)}) copy-start(f32[320,1024]{1,0:T(8,128)} %convolution_add_fusion.1) | copy-start | bytes 3932164
  293.5 7.2 %copy-start.3 = (f32[320,1024]{1,0:T(8,128)S(1)}, f32[320,1024]{1,0:T(8,128)}, u32[]{:S(2)}) copy-start(f32[320,1024]{1,0:T(8,128)} %convolution_add_fusion.2) | copy-start | bytes 3932164
  304.4 3.3 %copy-start = (f32[3,320,1024]{2,1,0:T(8,128)}, f32[3,320,1024]{2,1,0:T(8,128)S(1)}, u32[]{:S(2)}) copy-start(f32[3,320,1024]{2,1,0:T(8,128)S(1)} %pad_maximum_fusion.1) | copy-start | bytes 11796484
